TPU v7x, 256 devices: a whole 4x4x8 slice. The times are simulated.
256 devices in a mesh: req: 64 (over x, y, z_hi), mesh: 4 (over z_lo, core).
Axes of the slice: x: 4, y: 4, z: 8 (z_hi: 4, z_lo: 2; z = z_hi * 2 + z_lo), core: 2. Of those that a mesh axis runs over, the one named last changes fastest.
Arguments:
- tokens: bfloat16 [1024, 64, 1024], P(('req', 'mesh')), may hold values from -6 to 6
- lengths: int32 [1024], P(('req', 'mesh')), may hold values from 1 to 64, 49152 in all
- ridge_keys: float32 [1024, 8, 128, 128], P(('req', 'mesh')), as said below
- ridge_values: float32 [1024, 8, 128, 128], P(('req', 'mesh')), may hold values from -0.5 to 0.5
- conv_tail: bfloat16 [1024, 3, 3072], P(('req', 'mesh')), may hold values from -6 to 6
- page_table: int32 [1024], P(('req', 'mesh')), may hold values from 0 to 15, as said below
- w_qkv: bfloat16 [1024, 3072], P(('req', 'mesh')), may hold values from -0.1875 to 0.1875
- conv_weight: float32 [4, 3072], replicated, may hold values from -3 to 3
- w_gates: bfloat16 [1024, 16], replicated, may hold values from -0.1875 to 0.1875
- decay_rate: float32 [8], replicated, may hold values from 0.001 to 0.03
- ridge: float32 [8], replicated, may hold values from 0.01 to 0.1
- w_out: bfloat16 [1024, 1024], P(('req', 'mesh')), may hold values from -0.1875 to 0.1875
- attn_gain: float32 [1024], replicated, may hold values from 0.5 to 1.5
- ffn_gain: float32 [1024], replicated, may hold values from 0.5 to 1.5
- w_gate: bfloat16 [1024, 2816], P('req', 'mesh'), may hold values from -0.1875 to 0.1875
- w_up: bfloat16 [1024, 2816], P('req', 'mesh'), may hold values from -0.1875 to 0.1875
- w_down: bfloat16 [2816, 1024], P('mesh', 'req'), may hold values from -0.109375 to 0.109375
Outputs:
- mixed: bfloat16 [1024, 64, 1024], P(('req', 'mesh'))
- keys_decode: float32 [1024, 8, 128, 128], P(('req', 'mesh'))
- values_decode: float32 [1024, 8, 128, 128], P(('req', 'mesh'))
- tail_decode: bfloat16 [1024, 3, 3072], P(('req', 'mesh'))
- readout: bfloat16 [1024, 64, 1024], P(('req', 'mesh'))
Inputs may be any that keep to these rules, and one draw needn't show every extreme that they name: `page_table`: within each group of 16 consecutive requests the values are a permutation; value // 4 is a decode device of the group and value % 4 a slot on it, and the 4 requests of one device go to 4 different decode devices. `ridge_keys`: each matrix is symmetric with a positive diagonal that exceeds the sum of the magnitudes of its row's other entries.
All inputs are finite; a program needn't handle non-finite values. No bound on the sum of `lengths` on one device may be relied on, other than what follows from the above.
Results may differ from a plain program's by a relative error of at most 0.0095.
Values may be sent and summed in bfloat16 or wider, within the bound.
A program may use at most 128 MiB of HBM per device.

v0:
```python
import jax
import jax.numpy as jnp
from jax import lax
from jax.sharding import PartitionSpec as P

ITERS = 5


def rms_norm(values, gain):
    return values * lax.rsqrt(jnp.mean(values * values, axis=-1, keepdims=True) + 1e-05) * gain


def unit_rows(values):
    return values * lax.rsqrt(jnp.sum(values * values, axis=-1, keepdims=True) + 1e-06)


def prepare_heads(projected, gate_logits, conv_tail, lengths, conv_weight, decay_rate):
    requests, length, columns = projected.shape
    heads = decay_rate.shape[0]
    window = conv_tail.shape[1]
    extended = jnp.concatenate([conv_tail, projected], axis=1)
    conv_sum = jnp.zeros((requests, length, columns), jnp.float32)
    for tap_index in range(window + 1):
        conv_sum = conv_sum + conv_weight[tap_index] * extended[
            :, tap_index : tap_index + length
        ].astype(jnp.float32)
    activated = jax.nn.silu(conv_sum).reshape(requests, length, 3, heads, columns // (3 * heads))
    queries = unit_rows(activated[:, :, 0])
    keys_now = unit_rows(activated[:, :, 1])
    values_now = activated[:, :, 2]
    position = jnp.arange(length, dtype=jnp.int32)
    live = (position[None, :] < lengths[:, None]).astype(jnp.float32)[:, :, None]
    beta = jax.nn.sigmoid(gate_logits[..., 0]) * live
    log_decay = -decay_rate * jax.nn.softplus(gate_logits[..., 1]) * live
    new_tail = jax.vmap(
        lambda rows_all, first_row: lax.dynamic_slice_in_dim(rows_all, first_row, window, 0)
    )(extended, lengths)
    return (queries, keys_now, values_now, beta, log_decay, new_tail)


def mesa_core(
    queries, keys_now, values_now, beta, log_decay, keys_start, values_start, ridge, iterations
):
    highest = lax.Precision.HIGHEST
    cumulative = jnp.cumsum(jnp.swapaxes(log_decay, 1, 2), axis=-1)
    beta_heads = jnp.swapaxes(beta, 1, 2)
    length = cumulative.shape[-1]
    position = jnp.arange(length, dtype=jnp.int32)
    causal = position[:, None] >= position[None, :]
    spread = cumulative[..., :, None] - cumulative[..., None, :]
    weight = jnp.where(causal, jnp.exp(jnp.minimum(spread, 0.0)), 0.0) * beta_heads[..., None, :]
    carried = jnp.swapaxes(jnp.exp(cumulative), 1, 2)[..., None]
    ridge_term = ridge[None, None, :, None]
    solution = jnp.zeros_like(queries)
    residual = queries
    direction = queries
    res_norm = jnp.sum(residual * residual, axis=-1, keepdims=True)
    for step_index in range(iterations):
        start_part = carried * jnp.einsum(
            "bthj,bhij->bthi", direction, keys_start, precision=highest
        )
        apply_scores = (
            jnp.einsum("bthj,bshj->bhts", direction, keys_now, precision=highest) * weight
        )
        applied = (
            start_part
            + jnp.einsum("bhts,bshj->bthj", apply_scores, keys_now, precision=highest)
            + ridge_term * direction
        )
        step_size = res_norm / (jnp.sum(direction * applied, axis=-1, keepdims=True) + 1e-20)
        solution = solution + step_size * direction
        residual = residual - step_size * applied
        next_norm = jnp.sum(residual * residual, axis=-1, keepdims=True)
        direction = residual + next_norm / (res_norm + 1e-20) * direction
        res_norm = next_norm
    read_start = carried * jnp.einsum("bthj,bhij->bthi", solution, values_start, precision=highest)
    scores = jnp.einsum("bthj,bshj->bhts", solution, keys_now, precision=highest) * weight
    readout = read_start + jnp.einsum("bhts,bshj->bthj", scores, values_now, precision=highest)
    tail_weight = jnp.swapaxes(jnp.exp(cumulative[..., -1:] - cumulative) * beta_heads, 1, 2)[
        ..., None
    ]
    final_decay = jnp.exp(cumulative[..., -1])[..., None, None]
    keys_end = final_decay * keys_start + jnp.einsum(
        "bshi,bshj->bhij", keys_now * tail_weight, keys_now, precision=highest
    )
    values_end = final_decay * values_start + jnp.einsum(
        "bshi,bshj->bhij", values_now * tail_weight, keys_now, precision=highest
    )
    return (readout, keys_end, values_end)


def shards(
    tokens,
    lengths,
    ridge_keys,
    ridge_values,
    conv_tail,
    page_table,
    w_qkv,
    conv_weight,
    w_gates,
    decay_rate,
    ridge,
    w_out,
    attn_gain,
    ffn_gain,
    w_gate,
    w_up,
    w_down,
):
    highest = lax.Precision.HIGHEST
    requests, length, width = tokens.shape
    heads = decay_rate.shape[0]
    row_count = requests * length
    resident = tokens.astype(jnp.float32).reshape(row_count, width)
    normed = rms_norm(resident, attn_gain).astype(jnp.bfloat16)
    columns_in = normed
    projected = jnp.dot(
        columns_in,
        lax.all_gather(w_qkv, ("req", "mesh"), axis=0, tiled=True),
        preferred_element_type=jnp.float32,
    )
    projected = projected.astype(jnp.bfloat16).reshape(requests, length, -1)
    gate_logits = jnp.dot(normed, w_gates, preferred_element_type=jnp.float32).reshape(
        requests, length, heads, 2
    )
    queries, keys_now, values_now, beta, log_decay, new_tail = prepare_heads(
        projected, gate_logits, conv_tail, lengths, conv_weight, decay_rate
    )
    readout, keys_end, values_end = mesa_core(
        queries, keys_now, values_now, beta, log_decay, ridge_keys, ridge_values, ridge, ITERS
    )
    head_rows = readout.reshape(row_count, -1).astype(jnp.bfloat16)
    columns_in = head_rows
    attended = jnp.dot(
        columns_in,
        lax.all_gather(w_out, ("req", "mesh"), axis=0, tiled=True),
        preferred_element_type=jnp.float32,
    )
    after_attn = (resident + attended).astype(jnp.bfloat16)
    ffn_in = rms_norm(after_attn.astype(jnp.float32), ffn_gain).astype(jnp.bfloat16)
    group_tokens = lax.all_gather(ffn_in, "mesh", axis=0, tiled=True)
    columns_in = group_tokens
    gate_proj = jnp.dot(
        columns_in,
        lax.all_gather(w_gate, "req", axis=0, tiled=True),
        preferred_element_type=jnp.float32,
    )
    upward = jnp.dot(
        columns_in,
        lax.all_gather(w_up, "req", axis=0, tiled=True),
        preferred_element_type=jnp.float32,
    )
    hidden = (jax.nn.silu(gate_proj) * upward).astype(jnp.bfloat16)
    down_whole = lax.all_gather(w_down, "req", axis=1, tiled=True)
    ffn_out = lax.psum_scatter(
        jnp.dot(hidden, down_whole, preferred_element_type=jnp.float32).astype(jnp.bfloat16),
        "mesh",
        scatter_dimension=0,
        tiled=True,
    ).astype(jnp.float32)
    mixed = (
        (after_attn.astype(jnp.float32) + ffn_out)
        .astype(jnp.bfloat16)
        .reshape(requests, length, width)
    )
    peers = lax.axis_size("mesh")
    destination = page_table // requests
    slot_index = page_table % requests
    select = (destination[None, :] == jnp.arange(peers, dtype=jnp.int32)[:, None]).astype(
        jnp.float32
    )
    send_keys = jnp.einsum("ej,jhab->ehab", select, keys_end, precision=highest)
    send_values = jnp.einsum("ej,jhab->ehab", select, values_end, precision=highest)
    send_tail = jnp.einsum(
        "ej,jrc->erc", select, new_tail.astype(jnp.float32), precision=highest
    ).astype(jnp.bfloat16)
    send_slot = jnp.sum(jnp.where(select > 0.5, slot_index[None, :], 0), axis=1)
    got_keys, got_values, got_tail, got_slot = (
        lax.all_to_all(
            send_keys.astype(jnp.bfloat16), "mesh", split_axis=0, concat_axis=0, tiled=True
        ).astype(send_keys.dtype),
        lax.all_to_all(
            send_values.astype(jnp.bfloat16), "mesh", split_axis=0, concat_axis=0, tiled=True
        ).astype(send_values.dtype),
        lax.all_to_all(send_tail, "mesh", split_axis=0, concat_axis=0, tiled=True),
        lax.all_to_all(send_slot, "mesh", split_axis=0, concat_axis=0, tiled=True),
    )
    placing = (got_slot[None, :] == jnp.arange(requests, dtype=jnp.int32)[:, None]).astype(
        jnp.float32
    )
    keys_decode = jnp.einsum("si,ihab->shab", placing, got_keys, precision=highest)
    values_decode = jnp.einsum("si,ihab->shab", placing, got_values, precision=highest)
    tail_decode = jnp.einsum(
        "si,irc->src", placing, got_tail.astype(jnp.float32), precision=highest
    ).astype(jnp.bfloat16)
    return (mixed, keys_decode, values_decode, tail_decode, head_rows.reshape(requests, length, -1))


def solution(mesh):
    in_specs = (
        P(("req", "mesh"), None, None),
        P(("req", "mesh")),
        P(("req", "mesh"), None, None, None),
        P(("req", "mesh"), None, None, None),
        P(("req", "mesh"), None, None),
        P(("req", "mesh")),
        P(("req", "mesh"), None),
        P(),
        P(),
        P(),
        P(),
        P(("req", "mesh"), None),
        P(),
        P(),
        P("req", "mesh"),
        P("req", "mesh"),
        P("mesh", "req"),
    )
    out_specs = (
        P(("req", "mesh"), None, None),
        P(("req", "mesh"), None, None, None),
        P(("req", "mesh"), None, None, None),
        P(("req", "mesh"), None, None),
        P(("req", "mesh"), None, None),
    )
    return jax.shard_map(shards, mesh=mesh, in_specs=in_specs, out_specs=out_specs, check_vma=False)
```

profile of v0, /device:TPU:1, one launch (start us, length us, event | category | flops | bytes accessed | tf_op | source)
XLA Modules:
  0.0 583.6 jit_solution(5874164278874121975)
XLA Ops:
  17.6 102.5 %all-gather.19.cloned.1.call-done = bf16[256,4,1024]{2,1,0:T(4,128)(2,1)} async-done(((bf16[1,4,1024]{2,1,0:T(4,128)(2,1)}), bf16[256,4,1024]{2,1,0:T(4,128)(2,1)}) %all-gather.19.cloned.1.call-update) | async-done | bytes 2097168 | tf_op jit(solution)/shard_map/all_gather | solution.py:137
  120.0 3.9 reshape.219
  124.0 114.9 %all-gather.17.cloned.1.call-done = bf16[256,4,3072]{2,1,0:T(4,128)(2,1)} async-done(((bf16[1,4,3072]{2,1,0:T(4,128)(2,1)}), bf16[256,4,3072]{2,1,0:T(4,128)(2,1)}) %all-gather.17.cloned.1.call-update) | async-done | bytes 6291472 | tf_op jit(solution)/shard_map/all_gather | solution.py:120
  238.8 10.7 %reshape.217 = bf16[1024,3072]{1,0:T(8,128)(2,1)} reshape(bf16[256,4,3072]{2,1,0:T(4,128)(2,1)} %all-gather.17.cloned.1.call-done) | data formatting | bytes 12582912
  249.5 4.6 convolution_convert_fusion
  254.1 2.2 divide_multiply_fusion
  259.2 4.1 fusion.30
  263.3 2.2 convolution_multiply_fusion.5
  265.5 2.1 multiply_reduce_fusion.7
  272.2 4.1 fusion.27
  282.0 4.1 fusion.24
  290.9 4.3 fusion.21
  298.4 4.1 fusion.18
  306.2 2.4 multiply_add_fusion.2
  310.6 4.2 fusion.15
  321.2 3.4 all-to-all-start
  326.7 2.5 copy.96
  330.8 17.8 %all-gather.9.cloned.1.call-done = bf16[1024,1024]{1,0:T(8,128)(2,1)} async-done(((bf16[256,1024]{1,0:T(8,128)(2,1)}), bf16[1024,1024]{1,0:T(8,128)(2,1)}) %all-gather.9.cloned.1.call-update) | async-done | bytes 2097168 | tf_op jit(solution)/shard_map/all_gather | solution.py:142
  348.6 5.3 fusion.107
  353.9 73.4 %all-gather.13.cloned.1.call-done = bf16[1024,704]{1,0:T(8,128)(2,1)} async-done(((bf16[16,704]{1,0:T(8,128)(2,1)}), bf16[1024,704]{1,0:T(8,128)(2,1)}) %all-gather.13.cloned.1.call-update) | async-done | bytes 1441808 | tf_op jit(solution)/shard_map/all_gather | solution.py:151
  427.3 77.3 %all-gather.15.cloned.1.call-done = bf16[704,1024]{0,1:T(8,128)(2,1)} async-done(((bf16[704,16]{0,1:T(8,128)(2,1)}), bf16[704,1024]{0,1:T(8,128)(2,1)}) %all-gather.15.cloned.1.call-update) | async-done | bytes 1441808 | tf_op jit(solution)/shard_map/all_gather | solution.py:155
  504.6 8.2 %convolution_convert_fusion.3 = bf16[1024,1024]{1,0:T(8,128)(2,1)} fusion(bf16[704,1024]{0,1:T(8,128)(2,1)} %all-gather.15.cloned.1.call-done, f32[1024,704]{0,1:T(8,128)} %fusion.107, bf16[1024,1024]{1,0:T(8,128)(2,1)} %all-gather.9.cloned.1.call-done, bf16[1024,704]{1,0:T(8,128)(2,1)} %all-gather.13.cloned.1.call-done), kind=kOutput, calls=%fused_computation.16 | convolution fusion | flops 2958163968 | bytes 9961472 | tf_op jit(solution)/shard_map/dot_general | solution.py:157
  513.7 7.5 %multiply_add_fusion = f32[4,8,128,128]{3,2,1,0:T(8,128)} fusion(f32[4,8,128,128]{3,2,1,0:T(8,128)} %param.20, f32[4,8]{1,0:T(4,128)S(1)} %exp.47, f32[4,64,1,8,128]{4,3,2,1,0:T(8,128)} %copy-done.1, f32[4,64,8]{1,2,0:T(8,128)S(1)} %get-tuple-element.43, f32[4,64,1,8,128]{4,3,2,1,0:T(8,128)S(1)} %get-tuple-element.37, f32[4,64,8]{1,2,0:T(8,128)S(1)} %add_rsqrt_fusion), kind=kOutput, calls=%fused_computation.14 | convolution fusion | flops 404226048 | bytes 6307968 | tf_op jit(solution)/shard_map/bshi,bshj->bhij/dot_general | solution.py:86
  521.1 4.8 all-to-all-start.3
  525.9 4.9 fusion.11
  532.0 4.2 all-to-all-start.2
  536.3 4.7 multiply_add_fusion.1
  541.0 3.3 fusion.8
  545.5 8.5 %all-to-all-done.2 = bf16[4,8,128,128]{3,2,1,0:T(8,128)(2,1)} async-done(((bf16[4,8,128,128]{3,2,1,0:T(8,128)(2,1)}), bf16[4,8,128,128]{3,2,1,0:T(8,128)(2,1)}, u32[]{:S(2)}, u32[]{:S(2)}) %all-to-all-start.2) | async-done | bytes 1048608 | tf_op jit(solution)/shard_map/all_to_all | solution.py:183
  554.0 4.3 all-to-all-start.1
  560.1 2.1 fusion.41
  563.8 8.0 %all-to-all-done.1 = bf16[4,8,128,128]{3,2,1,0:T(8,128)(2,1)S(1)} async-done(((bf16[4,8,128,128]{3,2,1,0:T(8,128)(2,1)}), bf16[4,8,128,128]{3,2,1,0:T(8,128)(2,1)S(1)}, u32[]{:S(2)}, u32[]{:S(2)}) %all-to-all-start.1) | async-done | bytes 1048608 | tf_op jit(solution)/shard_map/all_to_all | solution.py:180
  (120 shorter events, 57.9 us)
Async XLA Ops:
  7.2 9.4 %copy-start.8 = (bf16[4,64,1024]{2,1,0:T(8,128)(2,1)S(1)}, bf16[4,64,1024]{2,1,0:T(8,128)(2,1)}, u32[]{:S(2)}) copy-start(bf16[4,64,1024]{2,1,0:T(8,128)(2,1)} %param.17) | copy-start | bytes 1572868
  7.2 10.2 %copy-start.11 = (bf16[4,3,3072]{2,0,1:T(4,128)(2,1)S(1)}, bf16[4,3,3072]{2,0,1:T(4,128)(2,1)}, u32[]{:S(2)}) copy-start(bf16[4,3,3072]{2,0,1:T(4,128)(2,1)} %param.21) | copy-start | bytes 221188
  7.2 112.8 %all-gather.19.cloned.1.call-start = ((), (), s32[]{:S(2)}) async-start(), calls=%async_computation.11 | async-start | bytes 2105344 | tf_op jit(solution)/shard_map/all_gather | solution.py:137
  7.9 230.9 %all-gather.17.cloned.1.call-start = ((), (), s32[]{:S(2)}) async-start(), calls=%async_computation.10 | async-start | bytes 6316032 | tf_op jit(solution)/shard_map/all_gather | solution.py:120
  8.7 322.1 %all-gather.11.cloned.1.call-start = ((), (), s32[]{:S(2)}) async-start(), calls=%async_computation.6 | async-start | bytes 1597440 | tf_op jit(solution)/shard_map/all_gather | solution.py:146
  9.4 339.2 %all-gather.9.cloned.1.call-start = ((), (), s32[]{:S(2)}) async-start(), calls=%async_computation.5 | async-start | bytes 2621440 | tf_op jit(solution)/shard_map/all_gather | solution.py:142
  254.1 2.3 copy-start.3
  257.2 57.6 %copy-start.1 = (f32[4,64,1,8,128]{4,3,2,1,0:T(8,128)}, f32[4,64,1,8,128]{4,3,2,1,0:T(8,128)S(1)}, u32[]{:S(2)}) copy-start(f32[4,64,1,8,128]{4,3,2,1,0:T(8,128)S(1)} %get-tuple-element.36) | copy-start | bytes 3145732
  257.2 2.0 copy-start
  263.3 2.2 copy-start.12
  308.5 2.0 copy-start.2
  314.8 1.7 copy-start.9
  314.8 1.8 copy-start.10
  316.1 1.3 copy-start.4
  316.5 1.6 copy-start.13
  316.5 3.8 copy-start.15
  316.5 8.2 %copy-start.14 = (s32[4]{0:T(128)S(1)}, s32[4]{0:T(128)}, u32[]{:S(2)}) copy-start(s32[4]{0:T(128)} %param.18) | copy-start | bytes 52
  317.4 0.8 copy-start.6
  319.2 108.1 %all-gather.13.cloned.1.call-start = ((), (), s32[]{:S(2)}) async-start(), calls=%async_computation.7 | async-start | bytes 1597440 | tf_op jit(solution)/shard_map/all_gather | solution.py:151
  319.8 184.8 %all-gather.15.cloned.1.call-start = ((), (), s32[]{:S(2)}) async-start(), calls=%async_computation.8 | async-start | bytes 1597440 | tf_op jit(solution)/shard_map/all_gather | solution.py:155
  321.2 199.9 %all-to-all-start = ((s32[4,1,1]{2,1,0:T(1,128)}), s32[4,1,1]{2,1,0:T(1,128)S(1)}, u32[]{:S(2)}, u32[]{:S(2)}) async-start(s32[4,1,1]{2,1,0:T(1,128)} %copy.89), calls=%async_computation.1 | async-start | bytes 4096 | tf_op jit(solution)/shard_map/all_to_all | solution.py:187
  324.6 249.7 %reduce-scatter.2.cloned.1.call-start = ((), (), s32[]{:S(2)}) async-start(), calls=%async_computation.9 | async-start | bytes 2621440 | tf_op jit(solution)/shard_map/reduce_scatter | solution.py:156
  521.1 10.9 %all-to-all-start.3 = ((bf16[4,3,3072]{2,1,0:T(4,128)(2,1)}), bf16[4,3,3072]{2,1,0:T(4,128)(2,1)S(1)}, u32[]{:S(2)}, u32[]{:S(2)}) async-start(bf16[4,3,3072]{2,1,0:T(4,128)(2,1)} %copy.97), calls=%async_computation.4 | async-start | bytes 196608 | tf_op jit(solution)/shard_map/all_to_all | solution.py:186
  532.0 22.0 %all-to-all-start.2 = ((bf16[4,8,128,128]{3,2,1,0:T(8,128)(2,1)}), bf16[4,8,128,128]{3,2,1,0:T(8,128)(2,1)}, u32[]{:S(2)}, u32[]{:S(2)}) async-start(bf16[4,8,128,128]{3,2,1,0:T(8,128)(2,1)} %copy.94), calls=%async_computation.3 | async-start | bytes 2097152 | tf_op jit(solution)/shard_map/all_to_all | solution.py:183
  544.3 14.1 %copy-start.5 = (bf16[4,64,8,128]{3,1,2,0:T(8,128)(2,1)S(1)}, bf16[4,64,8,128]{3,1,2,0:T(8,128)(2,1)}, u32[]{:S(2)}) copy-start(bf16[4,64,8,128]{3,1,2,0:T(8,128)(2,1)} %copy-done.4) | copy-start | bytes 1572868
  554.0 17.8 %all-to-all-start.1 = ((bf16[4,8,128,128]{3,2,1,0:T(8,128)(2,1)}), bf16[4,8,128,128]{3,2,1,0:T(8,128)(2,1)S(1)}, u32[]{:S(2)}, u32[]{:S(2)}) async-start(bf16[4,8,128,128]{3,2,1,0:T(8,128)(2,1)} %copy.91), calls=%async_computation.2 | async-start | bytes 2097152 | tf_op jit(solution)/shard_map/all_to_all | solution.py:180
  572.7 1.6 copy-start.7
Sparse Core Ops, SparseCore 0:
  11.8 108.2 all-gather.18
  123.9 114.9 all-gather.16
  242.1 72.7 all-gather.10
  319.3 29.2 all-gather.8
  351.7 75.5 all-gather.12
  430.4 74.1 all-gather.14
  512.9 34.4 reduce-scatter.1
where the time goes:
time: 594 us; the launch traced here: 584 us
  waiting for transfers between devices  405 us (68%)
  matrix products  92 us (15%)
  local copies, waits for them, and re-layouts  32 us (5%)
  other arithmetic  21.9 us (4%)
  starting transfers between devices  17.1 us (3%)
  between operations  15.2 us (3%)
    all_gather x1, waiting for transfers between devices, shards(): lax.all_gather(w_qkv, ('req', 'mesh'), axis=0, tiled=True)  115 us
    all_gather x1, waiting for transfers between devices, shards(): lax.all_gather(w_out, ('req', 'mesh'), axis=0, tiled=True)  102 us
    all_gather x1, waiting for transfers between devices, shards(): down_whole = lax.all_gather(w_down, 'req', axis=1, tiled=True)  77.3 us
    all_gather x1, waiting for transfers between devices, shards(): lax.all_gather(w_up, 'req', axis=0, tiled=True)  73.4 us
    dot_general x5, matrix products, mesa_core(): jnp.einsum('bthj,bhij->bthi', direction, keys_start, precision=highest)  20.9 us
    unnamed x38, local copies, waits for them, and re-layouts  20.7 us
    all_gather x1, waiting for transfers between devices, shards(): group_tokens = lax.all_gather(ffn_in, 'mesh', axis=0, tiled=True)  17.8 us
  transfers between devices with their start and end apart: 11, of which 7 were waited for; matrix products, arithmetic and copies ran while one was open for 24% of the time, Pallas kernels for 0%

commit v1 on v0

--- a/solution.py
+++ b/solution.py
@@ -4,6 +4,11 @@
 from jax.sharding import PartitionSpec as P
 
 ITERS = 5
+
+
+def all_by_exchange(array, name, dim):
+    stack = jnp.stack([array] * lax.axis_size(name))
+    return jnp.concatenate(lax.all_to_all(stack, name, 0, 0), axis=dim)
 
 
 def rms_norm(values, gain):
@@ -116,9 +121,7 @@
     normed = rms_norm(resident, attn_gain).astype(jnp.bfloat16)
     columns_in = normed
     projected = jnp.dot(
-        columns_in,
-        lax.all_gather(w_qkv, ("req", "mesh"), axis=0, tiled=True),
-        preferred_element_type=jnp.float32,
+        columns_in, all_by_exchange(w_qkv, ("req", "mesh"), 0), preferred_element_type=jnp.float32
     )
     projected = projected.astype(jnp.bfloat16).reshape(requests, length, -1)
     gate_logits = jnp.dot(normed, w_gates, preferred_element_type=jnp.float32).reshape(

time: 594 us -> 522 us (0.88); the launches traced: 584 us -> 518 us
  waiting for transfers between devices: 405 us -> 324 us
  starting transfers between devices: 17.1 us -> 33.5 us
    all_gather x1 -> x0, waiting for transfers between devices: 115 us -> none  [shards(): lax.all_gather(w_qkv, ('req', 'mesh'), axis=0, tiled=True)]
    all_gather x1, waiting for transfers between devices: 102 us -> 127 us  [shards(): lax.all_gather(w_out, ('req', 'mesh'), axis=0, tiled=True)]
    all_to_all x0 -> x1, starting transfers between devices: none -> 16.5 us  [all_by_exchange(): return jnp.concatenate(lax.all_to_all(stack, name, 0, 0), axis=dim)]
    all_to_all x0 -> x1, waiting for transfers between devices: none -> 13.9 us  [all_by_exchange(): return jnp.concatenate(lax.all_to_all(stack, name, 0, 0), axis=dim)]
    unnamed x38 -> x45, local copies, waits for them, and re-layouts: 20.7 us -> 9.92 us
    reshape x0 -> x1, local copies, waits for them, and re-layouts: none -> 10.6 us  [all_by_exchange(): return jnp.concatenate(lax.all_to_all(stack, name, 0, 0), axis=dim)]
  transfers between devices with their start and end apart: 11 -> 11, of which waited for: 7 -> 7; matrix products, arithmetic and copies ran while one was open for 24% -> 26% of each run, Pallas kernels for 0% -> 0%
where the time goes in v1:
time: 522 us; the launch traced here: 518 us
  waiting for transfers between devices  324 us (62%)
  matrix products  90.8 us (17%)
  local copies, waits for them, and re-layouts  35.3 us (7%)
  starting transfers between devices  33.5 us (6%)
  other arithmetic  19.3 us (4%)
  between operations  15.1 us (3%)
    all_gather x1, waiting for transfers between devices, shards(): lax.all_gather(w_out, ('req', 'mesh'), axis=0, tiled=True)  127 us
    all_gather x1, waiting for transfers between devices, shards(): down_whole = lax.all_gather(w_down, 'req', axis=1, tiled=True)  77.3 us
    all_gather x1, waiting for transfers between devices, shards(): lax.all_gather(w_up, 'req', axis=0, tiled=True)  73.4 us
    dot_general x5, matrix products, mesa_core(): jnp.einsum('bthj,bhij->bthi', direction, keys_start, precision=highest)  20.9 us
    all_to_all x1, starting transfers between devices, all_by_exchange(): return jnp.concatenate(lax.all_to_all(stack, name, 0, 0), axis=dim)  16.5 us
    all_to_all x1, waiting for transfers between devices, all_by_exchange(): return jnp.concatenate(lax.all_to_all(stack, name, 0, 0), axis=dim)  13.9 us
    all_gather x1, waiting for transfers between devices, shards(): group_tokens = lax.all_gather(ffn_in, 'mesh', axis=0, tiled=True)  13.5 us
    reshape x1, local copies, waits for them, and re-layouts, all_by_exchange(): return jnp.concatenate(lax.all_to_all(stack, name, 0, 0), axis=dim)  10.6 us
  transfers between devices with their start and end apart: 11, of which 7 were waited for; matrix products, arithmetic and copies ran while one was open for 26% of the time, Pallas kernels for 0%

profile of v1, /device:TPU:1, one launch (start us, length us, event | category | flops | bytes accessed | tf_op | source)
XLA Modules:
  0.0 517.7 jit_solution(5686953158112002258)
XLA Ops:
  7.2 5.0 stack.2
  12.2 16.5 %all-to-all-start = ((bf16[256,4,3072]{2,1,0:T(4,128)(2,1)}), bf16[256,4,3072]{2,1,0:T(4,128)(2,1)}, u32[]{:S(2)}, u32[]{:S(2)}) async-start(bf16[256,4,3072]{2,1,0:T(4,128)(2,1)} %stack.2), calls=%async_computation | async-start | bytes 12582912 | tf_op jit(solution)/shard_map/all_to_all | solution.py:11
  32.8 126.6 %all-gather.15.cloned.1.call-done = bf16[256,4,1024]{2,1,0:T(4,128)(2,1)} async-done(((bf16[1,4,1024]{2,1,0:T(4,128)(2,1)}), bf16[256,4,1024]{2,1,0:T(4,128)(2,1)}) %all-gather.15.cloned.1.call-update) | async-done | bytes 2097168 | tf_op jit(solution)/shard_map/all_gather | solution.py:140
  159.4 3.9 reshape.227
  163.3 13.9 %all-to-all-done = bf16[256,4,3072]{2,1,0:T(4,128)(2,1)} async-done(((bf16[256,4,3072]{2,1,0:T(4,128)(2,1)}), bf16[256,4,3072]{2,1,0:T(4,128)(2,1)}, u32[]{:S(2)}, u32[]{:S(2)}) %all-to-all-start) | async-done | bytes 6291488 | tf_op jit(solution)/shard_map/all_to_all | solution.py:11
  177.2 10.6 %reshape.211 = bf16[1024,3072]{1,0:T(8,128)(2,1)} reshape(bf16[256,4,3072]{2,1,0:T(4,128)(2,1)} %all-to-all-done) | data formatting | bytes 12582912 | tf_op jit(solution)/shard_map/reshape | solution.py:11
  187.9 4.6 convolution_convert_fusion
  192.5 2.2 divide_multiply_fusion
  197.5 4.1 fusion.30
  201.6 2.2 convolution_multiply_fusion.5
  210.7 4.1 fusion.27
  220.4 4.1 fusion.24
  229.3 4.3 fusion.21
  236.8 4.1 fusion.18
  244.6 2.4 multiply_add_fusion.2
  249.0 4.2 fusion.15
  259.5 3.2 all-to-all-start.1
  265.0 2.5 copy.96
  269.2 13.5 %all-gather.7.cloned.1.call-done = bf16[1024,1024]{1,0:T(8,128)(2,1)} async-done(((bf16[256,1024]{1,0:T(8,128)(2,1)}), bf16[1024,1024]{1,0:T(8,128)(2,1)}) %all-gather.7.cloned.1.call-update) | async-done | bytes 2097168 | tf_op jit(solution)/shard_map/all_gather | solution.py:145
  282.8 5.3 %fusion.104 = f32[1024,704]{0,1:T(8,128)} fusion(bf16[1024,1024]{1,0:T(8,128)(2,1)} %all-gather.7.cloned.1.call-done, bf16[1024,704]{1,0:T(8,128)(2,1)} %all-gather.9.cloned.1.call-done), kind=kOutput, calls=%fused_computation.173 | convolution fusion | flops 1476395008 | bytes 6422528 | tf_op jit(solution)/shard_map/dot_general | solution.py:147
  288.1 73.4 %all-gather.11.cloned.1.call-done = bf16[1024,704]{1,0:T(8,128)(2,1)} async-done(((bf16[16,704]{1,0:T(8,128)(2,1)}), bf16[1024,704]{1,0:T(8,128)(2,1)}) %all-gather.11.cloned.1.call-update) | async-done | bytes 1441808 | tf_op jit(solution)/shard_map/all_gather | solution.py:154
  361.5 77.3 %all-gather.13.cloned.1.call-done = bf16[704,1024]{0,1:T(8,128)(2,1)} async-done(((bf16[704,16]{0,1:T(8,128)(2,1)}), bf16[704,1024]{0,1:T(8,128)(2,1)}) %all-gather.13.cloned.1.call-update) | async-done | bytes 1441808 | tf_op jit(solution)/shard_map/all_gather | solution.py:158
  438.8 8.2 %convolution_convert_fusion.3 = bf16[1024,1024]{1,0:T(8,128)(2,1)} fusion(bf16[704,1024]{0,1:T(8,128)(2,1)} %all-gather.13.cloned.1.call-done, f32[1024,704]{0,1:T(8,128)} %fusion.104, bf16[1024,1024]{1,0:T(8,128)(2,1)} %all-gather.7.cloned.1.call-done, bf16[1024,704]{1,0:T(8,128)(2,1)} %all-gather.11.cloned.1.call-done), kind=kOutput, calls=%fused_computation.16 | convolution fusion | flops 2958163968 | bytes 9961472 | tf_op jit(solution)/shard_map/dot_general | solution.py:160
  447.9 7.5 %multiply_add_fusion = f32[4,8,128,128]{3,2,1,0:T(8,128)} fusion(f32[4,8,128,128]{3,2,1,0:T(8,128)} %param.20, f32[4,8]{1,0:T(4,128)S(1)} %exp.47, f32[4,64,1,8,128]{4,3,2,1,0:T(8,128)} %copy-done.1, f32[4,64,8]{1,2,0:T(8,128)S(1)} %get-tuple-element.43, f32[4,64,1,8,128]{4,3,2,1,0:T(8,128)S(1)} %get-tuple-element.37, f32[4,64,8]{1,2,0:T(8,128)S(1)} %add_rsqrt_fusion), kind=kOutput, calls=%fused_computation.14 | convolution fusion | flops 404226048 | bytes 6307968 | tf_op jit(solution)/shard_map/bshi,bshj->bhij/dot_general | solution.py:91
  455.3 4.8 all-to-all-start.4
  460.1 4.9 fusion.11
  466.2 4.2 all-to-all-start.3
  470.5 4.7 multiply_add_fusion.1
  475.1 3.3 fusion.8
  479.7 8.5 %all-to-all-done.3 = bf16[4,8,128,128]{3,2,1,0:T(8,128)(2,1)} async-done(((bf16[4,8,128,128]{3,2,1,0:T(8,128)(2,1)}), bf16[4,8,128,128]{3,2,1,0:T(8,128)(2,1)}, u32[]{:S(2)}, u32[]{:S(2)}) %all-to-all-start.3) | async-done | bytes 1048608 | tf_op jit(solution)/shard_map/all_to_all | solution.py:186
  488.2 4.3 all-to-all-start.2
  498.0 8.0 %all-to-all-done.2 = bf16[4,8,128,128]{3,2,1,0:T(8,128)(2,1)S(1)} async-done(((bf16[4,8,128,128]{3,2,1,0:T(8,128)(2,1)}), bf16[4,8,128,128]{3,2,1,0:T(8,128)(2,1)S(1)}, u32[]{:S(2)}, u32[]{:S(2)}) %all-to-all-start.2) | async-done | bytes 1048608 | tf_op jit(solution)/shard_map/all_to_all | solution.py:183
  (127 shorter events, 56.0 us)
Async XLA Ops:
  12.2 18.1 %copy-start.11 = (bf16[4,3,3072]{2,0,1:T(4,128)(2,1)S(1)}, bf16[4,3,3072]{2,0,1:T(4,128)(2,1)}, u32[]{:S(2)}) copy-start(bf16[4,3,3072]{2,0,1:T(4,128)(2,1)} %param.21) | copy-start | bytes 221188
  12.2 18.2 %copy-start.13 = (bf16[1024,16]{0,1:T(8,128)(2,1)S(1)}, bf16[1024,16]{0,1:T(8,128)(2,1)}, u32[]{:S(2)}) copy-start(bf16[1024,16]{0,1:T(8,128)(2,1)} %param.25) | copy-start | bytes 98308
  12.2 18.2 %copy-start.18 = (f32[8]{0:T(128)S(1)}, f32[8]{0:T(128)}, u32[]{:S(2)}) copy-start(f32[8]{0:T(128)} %param.26) | copy-start | bytes 100
  12.2 18.2 %copy-start.9 = (bf16[4,64,1024]{2,1,0:T(8,128)(2,1)S(1)}, bf16[4,64,1024]{2,1,0:T(8,128)(2,1)}, u32[]{:S(2)}) copy-start(bf16[4,64,1024]{2,1,0:T(8,128)(2,1)} %param.17) | copy-start | bytes 1572868
  12.2 18.4 %copy-start.17 = (s32[4]{0:T(128)S(1)}, s32[4]{0:T(128)}, u32[]{:S(2)}) copy-start(s32[4]{0:T(128)} %param.18) | copy-start | bytes 52
  12.2 18.5 %copy-start.15 = (f32[1024]{0:T(1024)S(1)}, f32[1024]{0:T(1024)}, u32[]{:S(2)}) copy-start(f32[1024]{0:T(1024)} %param.29) | copy-start | bytes 12292
  12.2 165.0 %all-to-all-start = ((bf16[256,4,3072]{2,1,0:T(4,128)(2,1)}), bf16[256,4,3072]{2,1,0:T(4,128)(2,1)}, u32[]{:S(2)}, u32[]{:S(2)}) async-start(bf16[256,4,3072]{2,1,0:T(4,128)(2,1)} %stack.2), calls=%async_computation | async-start | bytes 12582912 | tf_op jit(solution)/shard_map/all_to_all | solution.py:11
  28.8 4.0 copy-start.12
  28.8 130.6 %all-gather.15.cloned.1.call-start = ((), (), s32[]{:S(2)}) async-start(), calls=%async_computation.11 | async-start | bytes 2105344 | tf_op jit(solution)/shard_map/all_gather | solution.py:140
  29.5 239.7 %all-gather.9.cloned.1.call-start = ((), (), s32[]{:S(2)}) async-start(), calls=%async_computation.7 | async-start | bytes 1597440 | tf_op jit(solution)/shard_map/all_gather | solution.py:149
  30.3 252.5 %all-gather.7.cloned.1.call-start = ((), (), s32[]{:S(2)}) async-start(), calls=%async_computation.6 | async-start | bytes 2621440 | tf_op jit(solution)/shard_map/all_gather | solution.py:145
  192.5 2.3 copy-start.3
  195.6 57.6 %copy-start.1 = (f32[4,64,1,8,128]{4,3,2,1,0:T(8,128)}, f32[4,64,1,8,128]{4,3,2,1,0:T(8,128)S(1)}, u32[]{:S(2)}) copy-start(f32[4,64,1,8,128]{4,3,2,1,0:T(8,128)S(1)} %get-tuple-element.36) | copy-start | bytes 3145732
  195.6 2.0 copy-start
  201.6 2.2 copy-start.14
  247.0 2.0 copy-start.2
  253.2 1.7 copy-start.8
  253.2 1.7 copy-start.10
  254.5 1.2 copy-start.4
  254.9 1.7 copy-start.16
  254.9 3.8 copy-start.19
  255.8 0.8 copy-start.6
  257.6 103.9 %all-gather.11.cloned.1.call-start = ((), (), s32[]{:S(2)}) async-start(), calls=%async_computation.8 | async-start | bytes 1597440 | tf_op jit(solution)/shard_map/all_gather | solution.py:154
  258.1 180.7 %all-gather.13.cloned.1.call-start = ((), (), s32[]{:S(2)}) async-start(), calls=%async_computation.9 | async-start | bytes 1597440 | tf_op jit(solution)/shard_map/all_gather | solution.py:158
  259.5 195.8 %all-to-all-start.1 = ((s32[4,1,1]{2,1,0:T(1,128)}), s32[4,1,1]{2,1,0:T(1,128)S(1)}, u32[]{:S(2)}, u32[]{:S(2)}) async-start(s32[4,1,1]{2,1,0:T(1,128)} %copy.89), calls=%async_computation.2 | async-start | bytes 4096 | tf_op jit(solution)/shard_map/all_to_all | solution.py:190
  262.8 245.7 %reduce-scatter.2.cloned.1.call-start = ((), (), s32[]{:S(2)}) async-start(), calls=%async_computation.10 | async-start | bytes 2621440 | tf_op jit(solution)/shard_map/reduce_scatter | solution.py:159
  455.3 10.9 %all-to-all-start.4 = ((bf16[4,3,3072]{2,1,0:T(4,128)(2,1)}), bf16[4,3,3072]{2,1,0:T(4,128)(2,1)S(1)}, u32[]{:S(2)}, u32[]{:S(2)}) async-start(bf16[4,3,3072]{2,1,0:T(4,128)(2,1)} %copy.97), calls=%async_computation.5 | async-start | bytes 196608 | tf_op jit(solution)/shard_map/all_to_all | solution.py:189
  466.2 22.0 %all-to-all-start.3 = ((bf16[4,8,128,128]{3,2,1,0:T(8,128)(2,1)}), bf16[4,8,128,128]{3,2,1,0:T(8,128)(2,1)}, u32[]{:S(2)}, u32[]{:S(2)}) async-start(bf16[4,8,128,128]{3,2,1,0:T(8,128)(2,1)} %copy.94), calls=%async_computation.4 | async-start | bytes 2097152 | tf_op jit(solution)/shard_map/all_to_all | solution.py:186
  478.5 14.1 %copy-start.5 = (bf16[4,64,8,128]{3,1,2,0:T(8,128)(2,1)S(1)}, bf16[4,64,8,128]{3,1,2,0:T(8,128)(2,1)}, u32[]{:S(2)}) copy-start(bf16[4,64,8,128]{3,1,2,0:T(8,128)(2,1)} %copy-done.4) | copy-start | bytes 1572868
  488.2 17.8 %all-to-all-start.2 = ((bf16[4,8,128,128]{3,2,1,0:T(8,128)(2,1)}), bf16[4,8,128,128]{3,2,1,0:T(8,128)(2,1)S(1)}, u32[]{:S(2)}, u32[]{:S(2)}) async-start(bf16[4,8,128,128]{3,2,1,0:T(8,128)(2,1)} %copy.91), calls=%async_computation.3 | async-start | bytes 2097152 | tf_op jit(solution)/shard_map/all_to_all | solution.py:183
  506.9 1.6 copy-start.7
Sparse Core Ops, SparseCore 0:
  33.3 126.0 all-gather.14
  162.7 75.3 all-gather.8
  257.7 25.0 all-gather.6
  285.9 75.5 all-gather.10
  364.6 74.1 all-gather.12
  447.1 34.4 reduce-scatter.1
